TPU v7x, 32 devices: a whole 2x2x4 slice. The times are simulated.
32 devices in a mesh: row: 8 (over z, core), col: 4 (over y, x).
Axes of the slice: x: 2, y: 2, z: 4, core: 2. Of those that a mesh axis runs over, the one named last changes fastest.
Arguments:
- grm_prior: float32 [1024, 1024], P('row', 'col'), may hold values from -0.6 to 0.6
- dosage_now: bfloat16 [1024, 4096], P('row', 'col'), may hold values from 0 to 2
- mask_now: int32 [1024, 4096], P('row', 'col'), may hold values 0 or 1
- dosage_prev: bfloat16 [1024, 256], P('row'), may hold values from 0 to 2
- mask_prev: int32 [1024, 256], P('row'), may hold values 0 or 1
- expression: bfloat16 [1024, 20480], P('row', 'col'), may hold values from -18 to 18
Outputs:
- grm_total: float32 [1024, 1024], P('row', 'col')
- assoc_score: float32 [256, 20480], P('row', 'col')
All inputs are finite; a program needn't handle non-finite values. No bound on the sum of `mask_now` or of `mask_prev` on one device may be relied on, other than what follows from the above.
Results may differ from a plain program's by a relative error of at most 0.0029.
Values may be sent and summed in bfloat16 or wider, within the bound.
A program may use at most 64 MiB of HBM per device.

v0:
```python
import math
import jax
import jax.numpy as jnp
from jax import lax
from jax.sharding import PartitionSpec as P

VARIANTS = 4096
epsilon = 1e-05


def spread(value, axis, source):
    kept = jnp.where(lax.axis_index(axis) == source, value, 0).astype(value.dtype)
    return lax.psum(kept, axis)


def local_sums(dosage, present):
    values = dosage.astype(jnp.float32)
    weight = present.astype(jnp.float32)
    return (values, weight, jnp.sum(weight, 0), jnp.sum(weight * values, 0))


def body(grm_prior, dosage_now, mask_now, dosage_prev, mask_prev, expression):
    samples_all = dosage_now.shape[0] * lax.axis_size("row")
    values_now, weight_now, seen_now, summed_now = local_sums(dosage_now, mask_now)
    values_prev, weight_prev, seen_prev, summed_prev = local_sums(dosage_prev, mask_prev)
    traits = expression.astype(jnp.float32)
    squares_trait = jnp.sum(traits * traits, 0)
    seen_now, summed_now, seen_prev, summed_prev, squares_trait = lax.psum(
        (seen_now, summed_now, seen_prev, summed_prev, squares_trait), "row"
    )
    observed_now = jnp.maximum(seen_now, 1.0)
    observed_prev = jnp.maximum(seen_prev, 1.0)
    offset_now = weight_now * (values_now - summed_now / observed_now)
    offset_prev = weight_prev * (values_prev - summed_prev / observed_prev)
    second_now, second_prev = lax.psum(
        (jnp.sum(offset_now * offset_now, 0), jnp.sum(offset_prev * offset_prev, 0)), "row"
    )
    spread_now = second_now / observed_now
    spread_prev = second_prev / observed_prev
    scaled = (offset_now * lax.rsqrt(spread_now + epsilon)).astype(jnp.bfloat16)
    own_panel = lax.all_gather(scaled, "col", axis=1, tiled=True)
    panels = lax.axis_size("row") // lax.axis_size("col")
    column = lax.axis_index("col")
    blocks = []
    for member in range(panels):
        remote = spread(own_panel, "row", column * panels + member)
        blocks.append(
            lax.dot_general(
                own_panel, remote, (((1,), (1,)), ((), ())), preferred_element_type=jnp.float32
            )
        )
    grm_total = grm_prior + jnp.concatenate(blocks, 1) / VARIANTS
    genotype = offset_prev.astype(jnp.bfloat16)
    out_rows = genotype.shape[1] // lax.axis_size("row")
    first_row = lax.axis_index("row") * out_rows
    cross_sum = lax.psum_scatter(
        lax.dot_general(
            genotype, expression, (((0,), (0,)), ((), ())), preferred_element_type=jnp.float32
        ),
        "row",
        scatter_dimension=0,
        tiled=True,
    )
    spread_rows = lax.dynamic_slice_in_dim(spread_prev, first_row, out_rows, 0)
    power = squares_trait / samples_all
    assoc_score = (
        cross_sum
        * lax.rsqrt(spread_rows + epsilon)[:, None]
        * lax.rsqrt(power + epsilon)[None, :]
        / math.sqrt(samples_all)
    )
    return (grm_total, assoc_score)


def solution(mesh):
    in_specs = (
        P("row", "col"),
        P("row", "col"),
        P("row", "col"),
        P("row", None),
        P("row", None),
        P("row", "col"),
    )
    out_specs = (P("row", "col"), P("row", "col"))
    return jax.shard_map(body, mesh=mesh, in_specs=in_specs, out_specs=out_specs, check_vma=False)
```

profile of v0, /device:TPU:0, one launch (start us, length us, event | category | flops | bytes accessed | tf_op | source)
XLA Modules:
  0.0 232.5 jit_solution(1334787050042367653)
XLA Ops:
  7.2 0.0 copy-start.2
  7.2 0.0 copy-start.4
  7.2 0.0 copy-start.1
  7.2 0.0 all-gather.2.cloned.1.call-start
  7.2 1.3 convert_reduce_fusion
  8.6 0.0 copy-start.3
  8.6 1.0 convert_reduce_fusion.1
  9.6 30.3 %all-reduce.1 = (f32[1024]{0:T(1024)S(1)}, f32[1024]{0:T(1024)S(1)}, f32[256]{0:T(256)S(1)}, f32[256]{0:T(256)S(1)}) all-reduce(f32[1024]{0:T(1024)S(1)} %get-tuple-element.5, f32[1024]{0:T(1024)S(1)} %get-tuple-element.4, f32[256]{0:T(256)S(1)} %get-tuple-element.7, ...), channel_id=1, replica_groups=mesh['row'=8,'col'=4] {'row'}, use_global_device_ids=true, to_apply=%region_1.0 | all-reduce | flops 2560 | bytes 20480 | tf_op jit(solution)/shard_map/psum | solution.py:28
  39.9 0.0 copy-done.2
  39.9 1.1 multiply_reduce_fusion.1
  41.0 0.0 copy-done.4
  41.0 0.9 multiply_reduce_fusion.2
  41.9 0.0 copy-done.1
  41.9 0.3 multiply_reduce_fusion
  42.2 26.0 %all-reduce = (f32[1024]{0:T(1024)S(1)}, f32[5120]{0:T(1024)S(1)}, f32[256]{0:T(256)S(1)}) all-reduce(f32[1024]{0:T(1024)S(1)} %multiply_reduce_fusion.1, f32[5120]{0:T(1024)S(1)} %multiply_reduce_fusion, f32[256]{0:T(256)S(1)} %multiply_reduce_fusion.2), channel_id=1, replica_groups=mesh['row'=8,'col'=4] {'row'}, use_global_device_ids=true, to_apply=%region_5.0 | all-reduce | flops 6400 | bytes 51200 | tf_op jit(solution)/shard_map/psum | solution.py:35
  68.2 0.0 copy-done.3
  68.2 0.8 multiply_convert_fusion
  69.0 0.0 all-gather.2.cloned.1.call-update
  69.0 0.0 all-reduce.5.cloned.1.call-start
  69.1 24.8 %all-gather.2.cloned.1.call-done = bf16[128,4096]{1,0:T(8,128)(2,1)} async-done(((bf16[128,1024]{1,0:T(8,128)(2,1)}), bf16[128,4096]{1,0:T(8,128)(2,1)}) %all-gather.2.cloned.1.call-update) | async-done | bytes 1048592 | tf_op jit(solution)/shard_map/all_gather | solution.py:41
  93.9 2.8 %broadcast_select_fusion.1 = (bf16[128,4096]{1,0:T(8,128)(2,1)}, bf16[128,4096]{1,0:T(8,128)(2,1)}) fusion(bf16[128,4096]{1,0:T(8,128)(2,1)} %all-gather.2.cloned.1.call-done, pred[]{:T(512)S(6)} %eq.6, pred[]{:T(512)S(6)} %eq.7), kind=kLoop, calls=%fused_computation.2 | loop fusion | flops 1048576 | bytes 3145730 | tf_op jit(solution)/shard_map/jit(_where)/select_n | solution.py:12
  96.6 0.0 copy-start.6
  96.6 0.0 all-reduce.5.cloned.1.call-update
  96.7 0.0 reduce-scatter.2.cloned.1.call-start
  96.7 0.8 copy-done.6
  97.5 3.2 %fusion.6 = f32[256,5120]{1,0:T(8,128)} fusion(bf16[128,5120]{1,0:T(8,128)(2,1)S(1)} %copy-done.1, bf16[128,256]{1,0:T(8,128)(2,1)S(1)} %copy-done.6, s32[128,256]{1,0:T(8,128)S(1)} %copy-done.4, f32[256]{0:T(256)S(1)} %maximum_divide_fusion.2), kind=kOutput, calls=%fused_computation.20 | convolution fusion | flops 335708160 | bytes 6751232 | tf_op jit(solution)/shard_map/dot_general | solution.py:57
  100.7 0.0 copy-start.7
  100.7 0.0 copy-start
  100.7 0.0 reduce-scatter.2.cloned.1.call-update
  100.7 0.9 copy-done.7
  101.6 0.1 copy.8
  101.7 0.1 add_rsqrt_fusion.2
  101.8 60.3 %all-reduce.5.cloned.1.call-done = (bf16[128,4096]{1,0:T(8,128)(2,1)}, bf16[128,4096]{1,0:T(8,128)(2,1)}) async-done(((bf16[128,4096]{1,0:T(8,128)(2,1)}, bf16[128,4096]{1,0:T(8,128)(2,1)}), (bf16[128,4096]{1,0:T(8,128)(2,1)}, bf16[128,4096]{1,0:T(8,128)(2,1)})) %all-reduce.5.cloned.1.call-update) | async-done | bytes 2097168 | tf_op jit(solution)/shard_map/psum | solution.py:13
  162.1 0.0 copy-start.5
  162.1 0.0 copy-done
  162.1 1.7 fusion.9
  163.8 0.0 copy-done.5
  163.8 0.5 fusion.10
  164.4 0.8 copy.9
  165.2 58.7 %reduce-scatter.2.cloned.1.call-done = f32[32,5120]{1,0:T(8,128)} async-done(((f32[256,5120]{1,0:T(8,128)}), f32[32,5120]{1,0:T(8,128)}) %reduce-scatter.2.cloned.1.call-update) | async-done | bytes 655376 | tf_op jit(solution)/shard_map/reduce_scatter | solution.py:56
  223.9 2.1 multiply_multiply_fusion
  (6 shorter events, 0.1 us)
Async XLA Ops:
  7.2 32.7 %copy-start.2 = (s32[128,1024]{1,0:T(8,128)S(1)}, s32[128,1024]{1,0:T(8,128)}, u32[]{:S(2)}) copy-start(s32[128,1024]{1,0:T(8,128)} %param.8) | copy-start | bytes 1572868
  7.2 33.8 %copy-start.4 = (s32[128,256]{1,0:T(8,128)S(1)}, s32[128,256]{1,0:T(8,128)}, u32[]{:S(2)}) copy-start(s32[128,256]{1,0:T(8,128)} %param.10) | copy-start | bytes 393220
  7.2 34.7 %copy-start.1 = (bf16[128,5120]{1,0:T(8,128)(2,1)S(1)}, bf16[128,5120]{1,0:T(8,128)(2,1)}, u32[]{:S(2)}) copy-start(bf16[128,5120]{1,0:T(8,128)(2,1)} %param.11) | copy-start | bytes 3932164
  7.2 86.7 %all-gather.2.cloned.1.call-start = ((), (), s32[]{:S(2)}) async-start(), calls=%async_computation.1 | async-start | bytes 1310720 | tf_op jit(solution)/shard_map/all_gather | solution.py:41
  8.6 59.6 %copy-start.3 = (bf16[128,1024]{1,0:T(8,128)(2,1)S(1)}, bf16[128,1024]{1,0:T(8,128)(2,1)}, u32[]{:S(2)}) copy-start(bf16[128,1024]{1,0:T(8,128)(2,1)} %param.7) | copy-start | bytes 786436
  69.0 93.1 %all-reduce.5.cloned.1.call-start = ((), (), s32[]{:S(2)}) async-start(), calls=%async_computation.3 | async-start | bytes 4194304 | tf_op jit(solution)/shard_map/psum | solution.py:13
  96.6 0.8 copy-start.6
  96.7 127.2 %reduce-scatter.2.cloned.1.call-start = ((), (), s32[]{:S(2)}) async-start(), calls=%async_computation.2 | async-start | bytes 5898240 | tf_op jit(solution)/shard_map/reduce_scatter | solution.py:56
  100.7 0.9 copy-start.7
  100.7 61.4 %copy-start = (bf16[128,4096]{1,0:T(8,128)(2,1)S(1)}, bf16[128,4096]{1,0:T(8,128)(2,1)}, u32[]{:S(2)}) copy-start(bf16[128,4096]{1,0:T(8,128)(2,1)} %all-gather.2.cloned.1.call-done) | copy-start | bytes 3145732
  162.1 1.8 copy-start.5
Sparse Core Ops, SparseCore 0:
  69.1 24.6 all-gather.1
  96.8 65.2 all-reduce.4
  164.4 59.4 reduce-scatter.1
where the time goes:
time: 233 us; the launch traced here: 232 us
  waiting for transfers between devices  144 us (62%)
  blocking collectives  56.3 us (24%)
  between operations  13.9 us (6%)
  other arithmetic  10.3 us (4%)
  matrix products  5.47 us (2%)
  local copies, waits for them, and re-layouts  2.51 us (1%)
    psum x1, waiting for transfers between devices, spread(): return lax.psum(kept, axis)  60.3 us
    reduce_scatter x1, waiting for transfers between devices, body(): lax.psum_scatter(lax.dot_general(genotype, expression, (((0,), (0,)), (()...  58.7 us
    psum x1, blocking collectives, body(): lax.psum((seen_now, summed_now, seen_prev, summed_prev, squares_trait), '...  30.3 us
    psum x1, blocking collectives, body(): lax.psum((jnp.sum(offset_now * offset_now, 0), jnp.sum(offset_prev * offs...  26 us
    all_gather x1, waiting for transfers between devices, body(): own_panel = lax.all_gather(scaled, 'col', axis=1, tiled=True)  24.8 us
  transfers between devices with their start and end apart: 3, of which 3 were waited for; matrix products, arithmetic and copies ran while one was open for 3% of the time, Pallas kernels for 0%

commit v1 on v0

--- a/solution.py
+++ b/solution.py
@@ -10,7 +10,7 @@
 
 def spread(value, axis, source):
     kept = jnp.where(lax.axis_index(axis) == source, value, 0).astype(value.dtype)
-    return lax.psum(kept, axis)
+    return lax.all_gather(kept, axis).sum(axis=0)
 
 
 def local_sums(dosage, present):

time: 233 us -> 310 us (1.33)
  waiting for transfers between devices: 144 us -> 212 us
  other arithmetic: 10.3 us -> 20.4 us
    all_gather x0 -> x2, waiting for transfers between devices: none -> 157 us  [spread(): return lax.all_gather(kept, axis).sum(axis=0)]
    psum x1 -> x0, waiting for transfers between devices: 60.3 us -> none  [spread(): return lax.psum(kept, axis)]
    reduce_scatter x1, waiting for transfers between devices: 58.7 us -> 32.9 us  [body(): lax.psum_scatter(lax.dot_general(genotype, expression, (((0,), (0,)), (()...]
    reduce_sum x0 -> x2, other arithmetic: none -> 9.9 us  [spread(): return lax.all_gather(kept, axis).sum(axis=0)]
    all_gather x1, waiting for transfers between devices: 24.8 us -> 21.5 us  [body(): own_panel = lax.all_gather(scaled, 'col', axis=1, tiled=True)]
  transfers between devices with their start and end apart: 3 -> 4, of which waited for: 3 -> 4; matrix products, arithmetic and copies ran while one was open for 3% -> 4% of each run, Pallas kernels for 0% -> 0%
where the time goes in v1:
time: 310 us
  waiting for transfers between devices  212 us (68%)
  blocking collectives  56.3 us (18%)
  other arithmetic  20.4 us (7%)
  between operations  15.8 us (5%)
  matrix products  4.05 us (1%)
    all_gather x2, waiting for transfers between devices, spread(): return lax.all_gather(kept, axis).sum(axis=0)  157 us
    reduce_scatter x1, waiting for transfers between devices, body(): lax.psum_scatter(lax.dot_general(genotype, expression, (((0,), (0,)), (()...  32.9 us
    psum x1, blocking collectives, body(): lax.psum((seen_now, summed_now, seen_prev, summed_prev, squares_trait), '...  30.3 us
    psum x1, blocking collectives, body(): lax.psum((jnp.sum(offset_now * offset_now, 0), jnp.sum(offset_prev * offs...  26 us
    all_gather x1, waiting for transfers between devices, body(): own_panel = lax.all_gather(scaled, 'col', axis=1, tiled=True)  21.5 us
    reduce_sum x2, other arithmetic, spread(): return lax.all_gather(kept, axis).sum(axis=0)  9.9 us
  transfers between devices with their start and end apart: 4, of which 4 were waited for; matrix products, arithmetic and copies ran while one was open for 4% of the time, Pallas kernels for 0%

profile of v1, /device:TPU:0, one launch (start us, length us, event | category | flops | bytes accessed | tf_op | source)
XLA Modules:
  0.0 309.5 jit_solution(14837297254893685724)
XLA Ops:
  8.0 0.0 copy-start.4
  8.0 0.0 copy-start.2
  8.0 0.0 copy-start.1
  8.0 0.0 copy-start.3
  8.0 0.0 copy-start.5
  8.1 0.0 all-gather.6.cloned.1.call-start
  8.1 1.1 convert_reduce_fusion.1
  9.2 1.2 convert_reduce_fusion
  10.4 30.3 %all-reduce.1 = (f32[1024]{0:T(1024)S(1)}, f32[1024]{0:T(1024)S(1)}, f32[256]{0:T(256)S(1)}, f32[256]{0:T(256)S(1)}) all-reduce(f32[1024]{0:T(1024)S(1)} %get-tuple-element.5, f32[1024]{0:T(1024)S(1)} %get-tuple-element.4, f32[256]{0:T(256)S(1)} %get-tuple-element.7, ...), channel_id=1, replica_groups=mesh['row'=8,'col'=4] {'row'}, use_global_device_ids=true, to_apply=%region_1.0 | all-reduce | flops 2560 | bytes 20480 | tf_op jit(solution)/shard_map/psum | solution.py:28
  40.7 1.0 multiply_reduce_fusion.2
  41.7 1.2 multiply_reduce_fusion.1
  42.9 0.0 copy-done.1
  43.0 0.3 multiply_reduce_fusion
  43.3 26.0 %all-reduce = (f32[1024]{0:T(1024)S(1)}, f32[5120]{0:T(1024)S(1)}, f32[256]{0:T(256)S(1)}) all-reduce(f32[1024]{0:T(1024)S(1)} %multiply_reduce_fusion.1, f32[5120]{0:T(1024)S(1)} %multiply_reduce_fusion, f32[256]{0:T(256)S(1)} %multiply_reduce_fusion.2), channel_id=1, replica_groups=mesh['row'=8,'col'=4] {'row'}, use_global_device_ids=true, to_apply=%region_5.0 | all-reduce | flops 6400 | bytes 51200 | tf_op jit(solution)/shard_map/psum | solution.py:35
  69.3 0.0 copy-done.2
  69.3 0.0 copy-done.3
  69.3 0.8 multiply_convert_fusion
  70.1 0.0 all-gather.6.cloned.1.call-update
  70.1 0.0 reduce-scatter.2.cloned.1.call-start
  70.2 0.0 copy-done.4
  70.2 0.0 copy-done.5
  70.2 3.2 %fusion.6 = f32[256,5120]{1,0:T(8,128)} fusion(bf16[128,5120]{1,0:T(8,128)(2,1)S(1)} %copy-done.1, bf16[128,256]{1,0:T(8,128)(2,1)S(1)} %copy-done.5, s32[128,256]{1,0:T(8,128)S(1)} %copy-done.4, f32[256]{0:T(256)S(1)} %maximum_divide_fusion.2), kind=kOutput, calls=%fused_computation.20 | convolution fusion | flops 335708160 | bytes 6751232 | tf_op jit(solution)/shard_map/dot_general | solution.py:57
  73.4 0.0 reduce-scatter.2.cloned.1.call-update
  73.4 0.0 all-gather.8.cloned.1.call-start
  73.5 0.0 copy-start.6
  73.5 21.5 %all-gather.6.cloned.1.call-done = bf16[128,4096]{1,0:T(8,128)(2,1)} async-done(((bf16[128,1024]{1,0:T(8,128)(2,1)}), bf16[128,4096]{1,0:T(8,128)(2,1)}) %all-gather.6.cloned.1.call-update) | async-done | bytes 1048592 | tf_op jit(solution)/shard_map/all_gather | solution.py:41
  95.0 2.7 broadcast_select_fusion.1
  97.7 0.0 all-gather.8.cloned.1.call-update
  97.7 0.0 all-gather.10.cloned.1.call-start
  97.7 0.5 all-gather.10.cloned.1.call-update
  98.3 0.0 copy-done.6
  98.3 0.1 copy.8
  98.4 0.1 add_rsqrt_fusion.2
  98.5 32.9 %reduce-scatter.2.cloned.1.call-done = f32[32,5120]{1,0:T(8,128)} async-done(((f32[256,5120]{1,0:T(8,128)}), f32[32,5120]{1,0:T(8,128)}) %reduce-scatter.2.cloned.1.call-update) | async-done | bytes 655376 | tf_op jit(solution)/shard_map/reduce_scatter | solution.py:56
  131.4 2.1 multiply_multiply_fusion
  133.5 79.9 %all-gather.8.cloned.1.call-done = bf16[1024,4096]{1,0:T(8,128)(2,1)} async-done(((bf16[128,4096]{1,0:T(8,128)(2,1)}), bf16[1024,4096]{1,0:T(8,128)(2,1)}) %all-gather.8.cloned.1.call-update) | async-done | bytes 8388624 | tf_op jit(solution)/shard_map/all_gather | solution.py:13
  213.3 4.9 %reduce_sum.90 = bf16[128,4096]{1,0:T(8,128)(2,1)S(1)} reduce(bf16[8,128,4096]{2,1,0:T(8,128)(2,1)} %bitcast.7, bf16[]{:T(256)} %constant.14.clone.1), dimensions={0}, to_apply=%region_6.0 | reduce | flops 3670016 | bytes 9437186 | tf_op jit(solution)/shard_map/reduce_sum | solution.py:13
  218.3 77.0 %all-gather.10.cloned.1.call-done = bf16[1024,4096]{1,0:T(8,128)(2,1)} async-done(((bf16[128,4096]{1,0:T(8,128)(2,1)}), bf16[1024,4096]{1,0:T(8,128)(2,1)}) %all-gather.10.cloned.1.call-update) | async-done | bytes 8388624 | tf_op jit(solution)/shard_map/all_gather | solution.py:13
  295.2 0.0 copy-start
  295.2 5.0 %reduce_sum.91 = bf16[128,4096]{1,0:T(8,128)(2,1)S(1)} reduce(bf16[8,128,4096]{2,1,0:T(8,128)(2,1)} %bitcast.8, bf16[]{:T(256)} %constant.14.clone.1), dimensions={0}, to_apply=%region_7.0 | reduce | flops 3670016 | bytes 9437186 | tf_op jit(solution)/shard_map/reduce_sum | solution.py:13
  300.2 0.0 copy-done
  300.2 0.4 fusion.9
  300.7 0.4 fusion.10
  301.2 0.8 copy.9
  (6 shorter events, 0.1 us)
Async XLA Ops:
  8.0 62.2 %copy-start.4 = (s32[128,256]{1,0:T(8,128)S(1)}, s32[128,256]{1,0:T(8,128)}, u32[]{:S(2)}) copy-start(s32[128,256]{1,0:T(8,128)} %param.10) | copy-start | bytes 393220
  8.0 61.3 %copy-start.2 = (s32[128,1024]{1,0:T(8,128)S(1)}, s32[128,1024]{1,0:T(8,128)}, u32[]{:S(2)}) copy-start(s32[128,1024]{1,0:T(8,128)} %param.8) | copy-start | bytes 1572868
  8.0 34.9 %copy-start.1 = (bf16[128,5120]{1,0:T(8,128)(2,1)S(1)}, bf16[128,5120]{1,0:T(8,128)(2,1)}, u32[]{:S(2)}) copy-start(bf16[128,5120]{1,0:T(8,128)(2,1)} %param.11) | copy-start | bytes 3932164
  8.0 61.2 %copy-start.3 = (bf16[128,1024]{1,0:T(8,128)(2,1)S(1)}, bf16[128,1024]{1,0:T(8,128)(2,1)}, u32[]{:S(2)}) copy-start(bf16[128,1024]{1,0:T(8,128)(2,1)} %param.7) | copy-start | bytes 786436
  8.0 62.1 %copy-start.5 = (bf16[128,256]{1,0:T(8,128)(2,1)S(1)}, bf16[128,256]{1,0:T(8,128)(2,1)}, u32[]{:S(2)}) copy-start(bf16[128,256]{1,0:T(8,128)(2,1)} %param.9) | copy-start | bytes 196612
  8.1 86.9 %all-gather.6.cloned.1.call-start = ((), (), s32[]{:S(2)}) async-start(), calls=%async_computation.1 | async-start | bytes 1310720 | tf_op jit(solution)/shard_map/all_gather | solution.py:41
  70.1 61.3 %reduce-scatter.2.cloned.1.call-start = ((), (), s32[]{:S(2)}) async-start(), calls=%async_computation.2 | async-start | bytes 5898240 | tf_op jit(solution)/shard_map/reduce_scatter | solution.py:56
  73.4 140.0 %all-gather.8.cloned.1.call-start = ((), (), s32[]{:S(2)}) async-start(), calls=%async_computation.3 | async-start | bytes 9437184 | tf_op jit(solution)/shard_map/all_gather | solution.py:13
  73.5 24.8 %copy-start.6 = (f32[128,256]{1,0:T(8,128)S(1)}, f32[128,256]{1,0:T(8,128)}, u32[]{:S(2)}) copy-start(f32[128,256]{1,0:T(8,128)} %param.6) | copy-start | bytes 393220
  97.7 197.5 %all-gather.10.cloned.1.call-start = ((), (), s32[]{:S(2)}) async-start(), calls=%async_computation.4 | async-start | bytes 9437184 | tf_op jit(solution)/shard_map/all_gather | solution.py:13
  295.2 5.0 %copy-start = (bf16[128,4096]{1,0:T(8,128)(2,1)S(1)}, bf16[128,4096]{1,0:T(8,128)(2,1)}, u32[]{:S(2)}) copy-start(bf16[128,4096]{1,0:T(8,128)(2,1)} %all-gather.6.cloned.1.call-done) | copy-start | bytes 3145732
Sparse Core Ops, SparseCore 0:
  70.2 24.6 all-gather.5
Sparse Core Ops, SparseCore 1:
  73.5 57.9 reduce-scatter.1
  132.9 80.4 all-gather.7
  214.8 80.4 all-gather.9
